TPU v7x, 32 devices: a whole 2x2x4 slice. The times are simulated.
32 devices in a mesh: uly: 2 (over y), blk: 16 (over z, x, core).
Axes of the slice: x: 2, y: 2, z: 4, core: 2. Of those that a mesh axis runs over, the one named last changes fastest.
Arguments:
- query_inputs: bfloat16 [4096, 2048], P(('blk', 'uly')), may hold values from -6 to 6
- key_inputs: bfloat16 [4096, 1024], P(('blk', 'uly')), may hold values from -6 to 6
- value_inputs: bfloat16 [4096, 1024], P(('blk', 'uly')), may hold values from -6 to 6
- forward_out: bfloat16 [4096, 2048], P(('blk', 'uly')), may hold values from -6 to 6
- output_gradient: bfloat16 [4096, 2048], P(('blk', 'uly')), may hold values from -4 to 4
- lse_parts: float32 [4096, 16, 2], P(('blk', 'uly')), may hold values from 3 to 247
- segment_ids: int32 [4096], P(('blk', 'uly')), may hold values from 0 to 31, never falling along the last dimension, each value on 1 to 512 neighbouring positions
Outputs:
- query_grad: bfloat16 [4096, 2048], P(('blk', 'uly'))
- key_grad: bfloat16 [4096, 1024], P(('blk', 'uly'))
- value_grad: bfloat16 [4096, 1024], P(('blk', 'uly'))
Inputs may be any that keep to these rules, and one draw needn't show every extreme that they name: `segment_ids`: never falls along the sequence; every document holds 1 to 512 tokens, and some document exactly 512.
All inputs are finite; a program needn't handle non-finite values.
Results may differ from a plain program's by a relative error of at most 0.0051.
Values may be sent and summed in bfloat16 or wider, within the bound.
A program may use at most 128 MiB of HBM per device.

v0:
```python
import math
import jax
import jax.numpy as jnp
from jax import lax
from jax.sharding import PartitionSpec as P

HEAD_SIZE = 128
QUERY_HEADS = 16
KEY_VALUE_HEADS = 8
HOPS = 2
QBLOCK = 512


def from_behind(block, axis, distance):
    devices = range(lax.axis_size(axis))
    route = [(i - distance, i) for i in devices if i - distance in devices]
    return lax.ppermute(block, axis, route)


def merge_parts(partials):
    highest = jnp.max(partials, axis=-1)
    return highest + jnp.log(jnp.sum(jnp.exp(partials - highest[..., None]), axis=-1))


def row_delta(grad_rows, out_rows):
    row_total = grad_rows.shape[0]
    products = grad_rows.astype(jnp.float32) * out_rows.astype(jnp.float32)
    return jnp.sum(products.reshape(row_total, -1, HEAD_SIZE), axis=-1)


def tile_grads(query_blk, grad_blk, lse_blk, delta_blk, key_blk, value_blk, allowed):
    score_scale = 1.0 / math.sqrt(HEAD_SIZE)
    scores = (
        jnp.einsum("mhgd,nhd->hgmn", query_blk, key_blk, preferred_element_type=jnp.float32)
        * score_scale
    )
    weights = jnp.where(allowed, jnp.exp(scores - lse_blk), 0.0)
    value_portion = jnp.einsum(
        "hgmn,mhgd->nhd", weights.astype(jnp.bfloat16), grad_blk, preferred_element_type=jnp.float32
    )
    prob_grad = jnp.einsum(
        "mhgd,nhd->hgmn", grad_blk, value_blk, preferred_element_type=jnp.float32
    )
    score_grad = (weights * (prob_grad - delta_blk)).astype(jnp.bfloat16)
    query_part = (
        jnp.einsum("hgmn,nhd->mhgd", score_grad, key_blk, preferred_element_type=jnp.float32)
        * score_scale
    )
    key_portion = (
        jnp.einsum("hgmn,mhgd->nhd", score_grad, query_blk, preferred_element_type=jnp.float32)
        * score_scale
    )
    return (query_part, key_portion, value_portion)


def per_device(
    query_inputs, key_inputs, value_inputs, forward_out, output_gradient, lse_parts, segment_ids
):
    uly_count = lax.axis_size("uly")
    blk_place = lax.axis_index("blk")
    tok_local = query_inputs.shape[0]
    row_count = tok_local * uly_count
    group_width = QUERY_HEADS // KEY_VALUE_HEADS
    query_loc, grad_loc, key_loc, value_loc, out_loc = (
        lax.all_to_all(query_inputs, "uly", split_axis=1, concat_axis=0, tiled=True),
        lax.all_to_all(output_gradient, "uly", split_axis=1, concat_axis=0, tiled=True),
        lax.all_to_all(key_inputs, "uly", split_axis=1, concat_axis=0, tiled=True),
        lax.all_to_all(value_inputs, "uly", split_axis=1, concat_axis=0, tiled=True),
        lax.all_to_all(forward_out, "uly", split_axis=1, concat_axis=0, tiled=True),
    )
    parts_loc = lax.all_to_all(
        lse_parts.reshape(tok_local, -1), "uly", split_axis=1, concat_axis=0, tiled=True
    )
    lse_loc = merge_parts(parts_loc.reshape(row_count, -1, 2))
    delta_loc = row_delta(grad_loc, out_loc)
    ids_loc = lax.all_gather(segment_ids, "uly", axis=0, tiled=True)
    kv_heads = key_loc.shape[1] // HEAD_SIZE
    query_quad = query_loc.reshape(row_count, kv_heads, group_width, HEAD_SIZE)
    gradient_quad = grad_loc.reshape(row_count, kv_heads, group_width, HEAD_SIZE)
    logsumexp_cube = lse_loc.reshape(row_count, kv_heads, group_width).transpose(1, 2, 0)[..., None]
    delta_cube = delta_loc.reshape(row_count, kv_heads, group_width).transpose(1, 2, 0)[..., None]
    key_cube = key_loc.reshape(row_count, kv_heads, HEAD_SIZE)
    value_cube = value_loc.reshape(row_count, kv_heads, HEAD_SIZE)
    rows_per_block = min(QBLOCK, row_count)
    block_total = row_count // rows_per_block
    position = jnp.arange(row_count, dtype=jnp.int32)
    query_parts = []
    key_gradient_running = jnp.zeros((row_count, kv_heads, HEAD_SIZE), jnp.float32)
    value_gradient_running = jnp.zeros((row_count, kv_heads, HEAD_SIZE), jnp.float32)
    for block_index in range(block_total):
        leading_row = block_index * rows_per_block
        finish = leading_row + rows_per_block
        allowed = (position[None, :finish] <= position[leading_row:finish, None]) & (
            ids_loc[None, :finish] == ids_loc[leading_row:finish, None]
        )
        tile_out = tile_grads(
            query_quad[leading_row:finish],
            gradient_quad[leading_row:finish],
            logsumexp_cube[:, :, leading_row:finish],
            delta_cube[:, :, leading_row:finish],
            key_cube[:finish],
            value_cube[:finish],
            allowed,
        )
        query_parts.append(tile_out[0])
        padding = ((0, row_count - finish), (0, 0), (0, 0))
        key_gradient_running = key_gradient_running + jnp.pad(tile_out[1], padding)
        value_gradient_running = value_gradient_running + jnp.pad(tile_out[2], padding)
    query_acc = jnp.concatenate(query_parts, axis=0)
    stacked_kv = jnp.stack([key_loc, value_loc])
    moved_kv = stacked_kv
    moved_ids = ids_loc
    key_parts = []
    for hop_index in range(1, HOPS + 1):
        moved_kv = from_behind(stacked_kv, "blk", hop_index)
        moved_ids = from_behind(ids_loc, "blk", hop_index)
        live = (blk_place >= hop_index) & (moved_ids[-1] == ids_loc[0])
        moved_key = moved_kv[0].reshape(row_count, kv_heads, HEAD_SIZE)
        moved_value = moved_kv[1].reshape(row_count, kv_heads, HEAD_SIZE)

        def compute_tile(unused):
            query_pieces = []
            key_sum = jnp.zeros((row_count, kv_heads, HEAD_SIZE), jnp.float32)
            value_sum = jnp.zeros((row_count, kv_heads, HEAD_SIZE), jnp.float32)
            for block_index in range(block_total):
                leading_row = block_index * rows_per_block
                finish = leading_row + rows_per_block
                allowed = moved_ids[None, :] == ids_loc[leading_row:finish, None]
                tile_out = tile_grads(
                    query_quad[leading_row:finish],
                    gradient_quad[leading_row:finish],
                    logsumexp_cube[:, :, leading_row:finish],
                    delta_cube[:, :, leading_row:finish],
                    moved_key,
                    moved_value,
                    allowed,
                )
                query_pieces.append(tile_out[0])
                key_sum = key_sum + tile_out[1]
                value_sum = value_sum + tile_out[2]
            stacked = jnp.stack([key_sum.reshape(row_count, -1), value_sum.reshape(row_count, -1)])
            return (jnp.concatenate(query_pieces, axis=0), stacked)

        def skip_tile(unused):
            return (
                jnp.zeros((row_count, kv_heads, group_width, HEAD_SIZE), jnp.float32),
                jnp.zeros((2, row_count, kv_heads * HEAD_SIZE), jnp.float32),
            )

        query_more, key_more = lax.cond(live, compute_tile, skip_tile, 0)
        query_acc = query_acc + query_more
        key_parts.append(key_more)
    returned = jnp.zeros((2, row_count, kv_heads * HEAD_SIZE), jnp.float32)
    for hop_index in range(1, HOPS + 1):
        returned = returned + from_behind(key_parts[hop_index - 1], "blk", -hop_index)
    key_total = (key_gradient_running.reshape(row_count, -1) + returned[0]).astype(jnp.bfloat16)
    value_total = (value_gradient_running.reshape(row_count, -1) + returned[1]).astype(jnp.bfloat16)
    query_total = query_acc.reshape(row_count, -1).astype(jnp.bfloat16)
    query_grad, key_grad, value_grad = (
        lax.all_to_all(query_total, "uly", split_axis=0, concat_axis=1, tiled=True),
        lax.all_to_all(key_total, "uly", split_axis=0, concat_axis=1, tiled=True),
        lax.all_to_all(value_total, "uly", split_axis=0, concat_axis=1, tiled=True),
    )
    return (query_grad, key_grad, value_grad)


def solution(mesh):
    placed = (
        P(("blk", "uly"), None),
        P(("blk", "uly"), None),
        P(("blk", "uly"), None),
        P(("blk", "uly"), None),
        P(("blk", "uly"), None),
        P(("blk", "uly"), None, None),
        P(("blk", "uly")),
    )
    return jax.shard_map(
        per_device,
        mesh=mesh,
        in_specs=placed,
        out_specs=(P(("blk", "uly"), None), P(("blk", "uly"), None), P(("blk", "uly"), None)),
        check_vma=False,
    )
```

profile of v0, /device:TPU:0, one launch (start us, length us, event | category | flops | bytes accessed | tf_op | source)
XLA Modules:
  0.0 147.4 jit_solution(7984379366214825627)
XLA Ops:
  0.7 4.4 %all-to-all-start.2 = ((f32[128,2,16]{0,2,1:T(8,128)}), f32[128,2,16]{0,2,1:T(8,128)S(1)}, u32[]{:S(2)}, u32[]{:S(2)}) async-start(f32[128,2,16]{0,2,1:T(8,128)} %bitcast.239), calls=%async_computation.2 | async-start | bytes 32768 | tf_op jit(solution)/shard_map/all_to_all | solution.py:71
  5.1 1.7 %copy.289 = bf16[16,2,8,512]{3,2,0,1:T(8,128)(2,1)} copy(bf16[16,2,8,512]{3,2,1,0:T(8,128)(2,1)} %bitcast.225) | data formatting | bytes 524288 | tf_op jit(solution)/shard_map/all_to_all | solution.py:67
  6.8 2.1 %all-to-all-done.2 = f32[128,2,16]{0,2,1:T(8,128)S(1)} async-done(((f32[128,2,16]{0,2,1:T(8,128)}), f32[128,2,16]{0,2,1:T(8,128)S(1)}, u32[]{:S(2)}, u32[]{:S(2)}) %all-to-all-start.2) | async-done | bytes 16416 | tf_op jit(solution)/shard_map/all_to_all | solution.py:71
  8.9 3.4 %all-to-all-start = ((bf16[128,2,512]{2,0,1:T(8,128)(2,1)}), bf16[128,2,512]{2,0,1:T(8,128)(2,1)S(1)}, u32[]{:S(2)}, u32[]{:S(2)}) async-start(bf16[128,2,512]{2,0,1:T(8,128)(2,1)} %bitcast.192), calls=%async_computation | async-start | bytes 524288 | tf_op jit(solution)/shard_map/all_to_all | solution.py:67
  12.4 1.7 %copy.288 = bf16[16,2,8,512]{3,2,0,1:T(8,128)(2,1)} copy(bf16[16,2,8,512]{3,2,1,0:T(8,128)(2,1)} %bitcast.226) | data formatting | bytes 524288 | tf_op jit(solution)/shard_map/all_to_all | solution.py:68
  14.1 3.4 %all-to-all-done = bf16[128,2,512]{2,0,1:T(8,128)(2,1)S(1)} async-done(((bf16[128,2,512]{2,0,1:T(8,128)(2,1)}), bf16[128,2,512]{2,0,1:T(8,128)(2,1)S(1)}, u32[]{:S(2)}, u32[]{:S(2)}) %all-to-all-start) | async-done | bytes 262176 | tf_op jit(solution)/shard_map/all_to_all | solution.py:67
  17.5 3.4 %all-to-all-start.3 = ((bf16[128,2,512]{2,0,1:T(8,128)(2,1)}), bf16[128,2,512]{2,0,1:T(8,128)(2,1)S(1)}, u32[]{:S(2)}, u32[]{:S(2)}) async-start(bf16[128,2,512]{2,0,1:T(8,128)(2,1)} %bitcast.191), calls=%async_computation.3 | async-start | bytes 524288 | tf_op jit(solution)/shard_map/all_to_all | solution.py:68
  21.0 5.2 %all-gather = s32[2,1,128]{2,1,0:T(1,128)S(1)} all-gather(s32[1,1,128]{2,1,0:T(1,128)S(1)} %bitcast.245), channel_id=1, replica_groups=mesh['uly'=2,'blk'=16] {'uly'}, dimensions={0}, use_global_device_ids=true | all-gather | bytes 1536 | tf_op jit(solution)/shard_map/all_gather | solution.py:76
  26.2 1.3 collective-permute-start
  27.5 4.5 %collective-permute-start.2 = (s32[256]{0:T(256)S(1)}, s32[256]{0:T(256)S(1)}, u32[]{:S(2)}, u32[]{:S(2)}) collective-permute-start(s32[256]{0:T(256)S(1)} %bitcast.234), channel_id=1, source_target_pairs={{0,2},{1,3},{2,4},{3,5},{4,6},{5,7},{6,8},{7,9},{8,10},{9,11},{10,... | collective-permute-start | bytes 3080 | tf_op jit(solution)/shard_map/ppermute | solution.py:17
  32.8 3.5 %all-to-all-start.4 = ((bf16[128,2,1024]{2,0,1:T(8,128)(2,1)}), bf16[128,2,1024]{2,0,1:T(8,128)(2,1)S(1)}, u32[]{:S(2)}, u32[]{:S(2)}) async-start(bf16[128,2,1024]{2,0,1:T(8,128)(2,1)} %bitcast.189), calls=%async_computation.4 | async-start | bytes 1048576 | tf_op jit(solution)/shard_map/all_to_all | solution.py:66
  42.6 2.7 %all-to-all-done.4 = bf16[128,2,1024]{2,0,1:T(8,128)(2,1)S(1)} async-done(((bf16[128,2,1024]{2,0,1:T(8,128)(2,1)}), bf16[128,2,1024]{2,0,1:T(8,128)(2,1)S(1)}, u32[]{:S(2)}, u32[]{:S(2)}) %all-to-all-start.4) | async-done | bytes 524320 | tf_op jit(solution)/shard_map/all_to_all | solution.py:66
  45.3 3.5 %all-to-all-start.5 = ((bf16[128,2,1024]{2,0,1:T(8,128)(2,1)}), bf16[128,2,1024]{2,0,1:T(8,128)(2,1)S(1)}, u32[]{:S(2)}, u32[]{:S(2)}) async-start(bf16[128,2,1024]{2,0,1:T(8,128)(2,1)} %bitcast.188), calls=%async_computation.5 | async-start | bytes 1048576 | tf_op jit(solution)/shard_map/all_to_all | solution.py:69
  49.9 2.9 %collective-permute-start.1 = (bf16[2,256,512]{1,2,0:T(8,128)(2,1)}, bf16[2,256,512]{1,2,0:T(8,128)(2,1)}, u32[]{:S(2)}, u32[]{:S(2)}) collective-permute-start(bf16[2,256,512]{1,2,0:T(8,128)(2,1)} %pad_maximum_fusion.2), channel_id=1, source_target_pairs={{0,1},{1,2},{2,3},{3,4},{4,5},{5,6},{6,7},{7,8},{8,9},{9,10},{10,1... | collective-permute-start | bytes 1572872 | tf_op jit(solution)/shard_map/ppermute | solution.py:17
  52.9 3.5 %collective-permute-start.3 = (bf16[2,256,512]{1,2,0:T(8,128)(2,1)}, bf16[2,256,512]{1,2,0:T(8,128)(2,1)}, u32[]{:S(2)}, u32[]{:S(2)}) collective-permute-start(bf16[2,256,512]{1,2,0:T(8,128)(2,1)} %pad_maximum_fusion.2), channel_id=1, source_target_pairs={{0,2},{1,3},{2,4},{3,5},{4,6},{5,7},{6,8},{7,9},{8,10},{9,11},{10,... | collective-permute-start | bytes 1572872 | tf_op jit(solution)/shard_map/ppermute | solution.py:17
  57.6 3.5 %all-to-all-start.1 = ((bf16[128,2,1024]{2,0,1:T(8,128)(2,1)}), bf16[128,2,1024]{2,0,1:T(8,128)(2,1)S(1)}, u32[]{:S(2)}, u32[]{:S(2)}) async-start(bf16[128,2,1024]{2,0,1:T(8,128)(2,1)} %bitcast.190), calls=%async_computation.1 | async-start | bytes 1048576 | tf_op jit(solution)/shard_map/all_to_all | solution.py:65
  61.9 8.2 %all-to-all-done.1 = bf16[128,2,1024]{2,0,1:T(8,128)(2,1)S(1)} async-done(((bf16[128,2,1024]{2,0,1:T(8,128)(2,1)}), bf16[128,2,1024]{2,0,1:T(8,128)(2,1)S(1)}, u32[]{:S(2)}, u32[]{:S(2)}) %all-to-all-start.1) | async-done | bytes 524320 | tf_op jit(solution)/shard_map/all_to_all | solution.py:65
  71.4 1.4 fusion.17
  72.9 2.2 %conditional.2 = (f32[256,4,2,128]{3,0,2,1:T(8,128)}, f32[2,256,512]{1,2,0:T(8,128)}) conditional(s32[]{:T(128)} %convert_element_type.56, () %tuple.24, (s32[256]{0:T(256)S(1)}, s32[256]{0:T(256)S(1)}, bf16[2,256,512]{1,2,0:T(8,128)(2,1)}, bf16[256,4,2,128]{3,2,1,0:T(2,128)(2,1)S(1)}, f32[4,2,256,1]{2,1,0,3:T(2,128)S(1)}, ...), branch_computations={%region_3.4_spmd, %region_4.5_spmd} | conditional | flops 675479552 | bytes 33441920 | solution.py:150
  75.0 1.3 collective-permute-start.4
  76.3 2.1 %conditional.3 = (f32[256,4,2,128]{3,0,2,1:T(8,128)}, f32[2,256,512]{1,2,0:T(8,128)}) conditional(s32[]{:T(128)} %convert_element_type.57, () %tuple.26, (s32[256]{0:T(256)S(1)}, s32[256]{0:T(256)S(1)}, bf16[2,256,512]{1,2,0:T(8,128)(2,1)}, bf16[256,4,2,128]{3,2,1,0:T(2,128)(2,1)S(1)}, f32[4,2,256,1]{2,1,0,3:T(2,128)S(1)}, ...), branch_computations={%region_5.6_spmd, %region_6.7_spmd} | conditional | flops 675479552 | bytes 33441920 | solution.py:150
  78.4 1.5 collective-permute-start.5
  79.9 1.6 %fusion.22 = f32[256,4,128]{2,0,1:T(8,128)S(1)} fusion(bf16[4,2,256,256]{2,3,1,0:T(8,128)(2,1)} %fusion.17, bf16[256,4,2,128]{3,2,1,0:T(2,128)(2,1)S(1)} %reshape.108), kind=kOutput, calls=%fused_computation.39 | convolution fusion | flops 134348800 | bytes 2097152 | tf_op jit(solution)/shard_map/hgmn,mhgd->nhd/dot_general | solution.py:50
  82.7 1.3 reshape.113
  86.1 1.7 %add_convert_fusion = bf16[256,4,2,128]{3,0,2,1:T(8,128)(2,1)S(1)} fusion(f32[256,4,2,128]{3,0,2,1:T(8,128)} %get-tuple-element.60, f32[256,4,2,128]{3,0,2,1:T(8,128)S(1)} %fusion.20, f32[256,4,2,128]{3,0,2,1:T(8,128)} %get-tuple-element.59), kind=kLoop, calls=%fused_computation.42 | loop fusion | flops 786432 | bytes 3670016 | tf_op jit(solution)/shard_map/convert_element_type | solution.py:158
  89.6 3.5 %all-to-all-start.6 = ((bf16[2,128,1024]{2,1,0:T(8,128)(2,1)}), bf16[2,128,1024]{2,1,0:T(8,128)(2,1)S(1)}, u32[]{:S(2)}, u32[]{:S(2)}) async-start(bf16[2,128,1024]{2,1,0:T(8,128)(2,1)} %convert_element_type.59), calls=%async_computation.6 | async-start | bytes 1048576 | tf_op jit(solution)/shard_map/all_to_all | solution.py:160
  93.1 32.8 %collective-permute-done.5 = f32[2,256,512]{1,2,0:T(8,128)} collective-permute-done((f32[2,256,512]{1,2,0:T(8,128)}, f32[2,256,512]{1,2,0:T(8,128)}, u32[]{:S(2)}, u32[]{:S(2)}) %collective-permute-start.5) | collective-permute-done | bytes 1048608 | tf_op jit(solution)/shard_map/ppermute | solution.py:17
  125.8 1.7 %add.28 = f32[2,256,512]{1,2,0:T(8,128)S(1)} add(f32[2,256,512]{1,2,0:T(8,128)} %collective-permute-done.4, f32[2,256,512]{1,2,0:T(8,128)} %collective-permute-done.5) | non-fusion elementwise | flops 262144 | bytes 3145728 | tf_op jit(solution)/shard_map/add | solution.py:155
  128.8 3.4 %all-to-all-start.7 = ((bf16[2,128,512]{2,1,0:T(8,128)(2,1)}), bf16[2,128,512]{2,1,0:T(8,128)(2,1)S(1)}, u32[]{:S(2)}, u32[]{:S(2)}) async-start(bf16[2,128,512]{2,1,0:T(8,128)(2,1)} %add_convert_fusion.2), calls=%async_computation.7 | async-start | bytes 524288 | tf_op jit(solution)/shard_map/all_to_all | solution.py:161
  133.0 4.7 %all-to-all-done.7 = bf16[2,128,512]{2,1,0:T(8,128)(2,1)S(1)} async-done(((bf16[2,128,512]{2,1,0:T(8,128)(2,1)}), bf16[2,128,512]{2,1,0:T(8,128)(2,1)S(1)}, u32[]{:S(2)}, u32[]{:S(2)}) %all-to-all-start.7) | async-done | bytes 262176 | tf_op jit(solution)/shard_map/all_to_all | solution.py:161
  137.7 3.4 %all-to-all-start.8 = ((bf16[2,128,512]{2,1,0:T(8,128)(2,1)}), bf16[2,128,512]{2,1,0:T(8,128)(2,1)S(1)}, u32[]{:S(2)}, u32[]{:S(2)}) async-start(bf16[2,128,512]{2,1,0:T(8,128)(2,1)} %add_convert_fusion.1), calls=%async_computation.8 | async-start | bytes 524288 | tf_op jit(solution)/shard_map/all_to_all | solution.py:162
  143.5 2.8 %all-to-all-done.8 = bf16[2,128,512]{2,1,0:T(8,128)(2,1)S(1)} async-done(((bf16[2,128,512]{2,1,0:T(8,128)(2,1)}), bf16[2,128,512]{2,1,0:T(8,128)(2,1)S(1)}, u32[]{:S(2)}, u32[]{:S(2)}) %all-to-all-start.8) | async-done | bytes 262176 | tf_op jit(solution)/shard_map/all_to_all | solution.py:162
  (68 shorter events, 23.4 us)
Async XLA Ops:
  0.6 20.4 %copy-start.13 = (s32[128]{0:T(128)S(1)}, s32[128]{0:T(128)}, u32[]{:S(2)}) copy-start(s32[128]{0:T(128)} %param.17) | copy-start | bytes 1540
  0.6 31.4 %copy-start.10 = (bf16[128,2048]{1,0:T(8,128)(2,1)S(1)}, bf16[128,2048]{1,0:T(8,128)(2,1)}, u32[]{:S(2)}) copy-start(bf16[128,2048]{1,0:T(8,128)(2,1)} %param.15) | copy-start | bytes 1572868
  0.7 8.3 %all-to-all-start.2 = ((f32[128,2,16]{0,2,1:T(8,128)}), f32[128,2,16]{0,2,1:T(8,128)S(1)}, u32[]{:S(2)}, u32[]{:S(2)}) async-start(f32[128,2,16]{0,2,1:T(8,128)} %bitcast.239), calls=%async_computation.2 | async-start | bytes 32768 | tf_op jit(solution)/shard_map/all_to_all | solution.py:71
  5.1 31.9 %copy-start.11 = (bf16[128,2048]{1,0:T(8,128)(2,1)S(1)}, bf16[128,2048]{1,0:T(8,128)(2,1)}, u32[]{:S(2)}) copy-start(bf16[128,2048]{1,0:T(8,128)(2,1)} %param.14) | copy-start | bytes 1572868
  8.9 8.6 %all-to-all-start = ((bf16[128,2,512]{2,0,1:T(8,128)(2,1)}), bf16[128,2,512]{2,0,1:T(8,128)(2,1)S(1)}, u32[]{:S(2)}, u32[]{:S(2)}) async-start(bf16[128,2,512]{2,0,1:T(8,128)(2,1)} %bitcast.192), calls=%async_computation | async-start | bytes 524288 | tf_op jit(solution)/shard_map/all_to_all | solution.py:67
  12.4 25.4 %copy-start.12 = (bf16[128,2048]{1,0:T(8,128)(2,1)S(1)}, bf16[128,2048]{1,0:T(8,128)(2,1)}, u32[]{:S(2)}) copy-start(bf16[128,2048]{1,0:T(8,128)(2,1)} %param.11) | copy-start | bytes 1572868
  17.5 15.3 %all-to-all-start.3 = ((bf16[128,2,512]{2,0,1:T(8,128)(2,1)}), bf16[128,2,512]{2,0,1:T(8,128)(2,1)S(1)}, u32[]{:S(2)}, u32[]{:S(2)}) async-start(bf16[128,2,512]{2,0,1:T(8,128)(2,1)} %bitcast.191), calls=%async_computation.3 | async-start | bytes 524288 | tf_op jit(solution)/shard_map/all_to_all | solution.py:68
  26.2 12.4 %collective-permute-start = (s32[256]{0:T(256)S(1)}, s32[256]{0:T(256)S(1)}, u32[]{:S(2)}, u32[]{:S(2)}) collective-permute-start(s32[256]{0:T(256)S(1)} %bitcast.233), channel_id=1, source_target_pairs={{0,1},{1,2},{2,3},{3,4},{4,5},{5,6},{6,7},{7,8},{8,9},{9,10},{10,1... | collective-permute-start | bytes 3080 | tf_op jit(solution)/shard_map/ppermute | solution.py:17
  27.5 13.0 %collective-permute-start.2 = (s32[256]{0:T(256)S(1)}, s32[256]{0:T(256)S(1)}, u32[]{:S(2)}, u32[]{:S(2)}) collective-permute-start(s32[256]{0:T(256)S(1)} %bitcast.234), channel_id=1, source_target_pairs={{0,2},{1,3},{2,4},{3,5},{4,6},{5,7},{6,8},{7,9},{8,10},{9,11},{10,... | collective-permute-start | bytes 3080 | tf_op jit(solution)/shard_map/ppermute | solution.py:17
  32.8 12.5 %all-to-all-start.4 = ((bf16[128,2,1024]{2,0,1:T(8,128)(2,1)}), bf16[128,2,1024]{2,0,1:T(8,128)(2,1)S(1)}, u32[]{:S(2)}, u32[]{:S(2)}) async-start(bf16[128,2,1024]{2,0,1:T(8,128)(2,1)} %bitcast.189), calls=%async_computation.4 | async-start | bytes 1048576 | tf_op jit(solution)/shard_map/all_to_all | solution.py:66
  45.3 12.3 %all-to-all-start.5 = ((bf16[128,2,1024]{2,0,1:T(8,128)(2,1)}), bf16[128,2,1024]{2,0,1:T(8,128)(2,1)S(1)}, u32[]{:S(2)}, u32[]{:S(2)}) async-start(bf16[128,2,1024]{2,0,1:T(8,128)(2,1)} %bitcast.188), calls=%async_computation.5 | async-start | bytes 1048576 | tf_op jit(solution)/shard_map/all_to_all | solution.py:69
  49.9 22.9 %collective-permute-start.1 = (bf16[2,256,512]{1,2,0:T(8,128)(2,1)}, bf16[2,256,512]{1,2,0:T(8,128)(2,1)}, u32[]{:S(2)}, u32[]{:S(2)}) collective-permute-start(bf16[2,256,512]{1,2,0:T(8,128)(2,1)} %pad_maximum_fusion.2), channel_id=1, source_target_pairs={{0,1},{1,2},{2,3},{3,4},{4,5},{5,6},{6,7},{7,8},{8,9},{9,10},{10,1... | collective-permute-start | bytes 1572872 | tf_op jit(solution)/shard_map/ppermute | solution.py:17
  52.9 23.5 %collective-permute-start.3 = (bf16[2,256,512]{1,2,0:T(8,128)(2,1)}, bf16[2,256,512]{1,2,0:T(8,128)(2,1)}, u32[]{:S(2)}, u32[]{:S(2)}) collective-permute-start(bf16[2,256,512]{1,2,0:T(8,128)(2,1)} %pad_maximum_fusion.2), channel_id=1, source_target_pairs={{0,2},{1,3},{2,4},{3,5},{4,6},{5,7},{6,8},{7,9},{8,10},{9,11},{10,... | collective-permute-start | bytes 1572872 | tf_op jit(solution)/shard_map/ppermute | solution.py:17
  57.6 12.5 %all-to-all-start.1 = ((bf16[128,2,1024]{2,0,1:T(8,128)(2,1)}), bf16[128,2,1024]{2,0,1:T(8,128)(2,1)S(1)}, u32[]{:S(2)}, u32[]{:S(2)}) async-start(bf16[128,2,1024]{2,0,1:T(8,128)(2,1)} %bitcast.190), calls=%async_computation.1 | async-start | bytes 1048576 | tf_op jit(solution)/shard_map/all_to_all | solution.py:65
  70.5 1.0 copy-start.9
  75.0 18.0 %collective-permute-start.4 = (f32[2,256,512]{1,2,0:T(8,128)}, f32[2,256,512]{1,2,0:T(8,128)}, u32[]{:S(2)}, u32[]{:S(2)}) collective-permute-start(f32[2,256,512]{1,2,0:T(8,128)} %get-tuple-element.61), channel_id=1, source_target_pairs={{1,0},{2,1},{3,2},{4,3},{5,4},{6,5},{7,6},{8,7},{9,8},{10,9},{11,1... | collective-permute-start | bytes 3145736 | tf_op jit(solution)/shard_map/ppermute | solution.py:17
  78.4 47.4 %collective-permute-start.5 = (f32[2,256,512]{1,2,0:T(8,128)}, f32[2,256,512]{1,2,0:T(8,128)}, u32[]{:S(2)}, u32[]{:S(2)}) collective-permute-start(f32[2,256,512]{1,2,0:T(8,128)} %get-tuple-element.62), channel_id=1, source_target_pairs={{2,0},{3,1},{4,2},{5,3},{6,4},{7,5},{8,6},{9,7},{10,8},{11,9},{12,... | collective-permute-start | bytes 3145736 | tf_op jit(solution)/shard_map/ppermute | solution.py:17
  84.4 1.2 copy-start.4
  89.6 39.2 %all-to-all-start.6 = ((bf16[2,128,1024]{2,1,0:T(8,128)(2,1)}), bf16[2,128,1024]{2,1,0:T(8,128)(2,1)S(1)}, u32[]{:S(2)}, u32[]{:S(2)}) async-start(bf16[2,128,1024]{2,1,0:T(8,128)(2,1)} %convert_element_type.59), calls=%async_computation.6 | async-start | bytes 1048576 | tf_op jit(solution)/shard_map/all_to_all | solution.py:160
  128.8 8.9 %all-to-all-start.7 = ((bf16[2,128,512]{2,1,0:T(8,128)(2,1)}), bf16[2,128,512]{2,1,0:T(8,128)(2,1)S(1)}, u32[]{:S(2)}, u32[]{:S(2)}) async-start(bf16[2,128,512]{2,1,0:T(8,128)(2,1)} %add_convert_fusion.2), calls=%async_computation.7 | async-start | bytes 524288 | tf_op jit(solution)/shard_map/all_to_all | solution.py:161
  137.7 8.6 %all-to-all-start.8 = ((bf16[2,128,512]{2,1,0:T(8,128)(2,1)}), bf16[2,128,512]{2,1,0:T(8,128)(2,1)S(1)}, u32[]{:S(2)}, u32[]{:S(2)}) async-start(bf16[2,128,512]{2,1,0:T(8,128)(2,1)} %add_convert_fusion.1), calls=%async_computation.8 | async-start | bytes 524288 | tf_op jit(solution)/shard_map/all_to_all | solution.py:162
where the time goes:
time: 149 us; the launch traced here: 147 us
  waiting for transfers between devices  56.8 us (38%)
  starting transfers between devices  47.1 us (32%)
  local copies, waits for them, and re-layouts  23.5 us (16%)
  other arithmetic  6.48 us (4%)
  blocking collectives  5.24 us (4%)
  matrix products  4.65 us (3%)
  between operations  3.64 us (2%)
    ppermute x6, waiting for transfers between devices, from_behind(): return lax.ppermute(block, axis, route)  32.8 us
    ppermute x6, starting transfers between devices, from_behind(): return lax.ppermute(block, axis, route)  14.9 us
    all_to_all x1, waiting for transfers between devices, per_device(): lax.all_to_all(query_inputs, 'uly', split_axis=1, concat_axis=0, tiled=True)  8.18 us
    all_gather x1, blocking collectives, per_device(): ids_loc = lax.all_gather(segment_ids, 'uly', axis=0, tiled=True)  5.24 us
    all_to_all x1, waiting for transfers between devices, per_device(): lax.all_to_all(key_total, 'uly', split_axis=0, concat_axis=1, tiled=True)  4.72 us
    all_to_all x1, starting transfers between devices, per_device(): lax.all_to_all(lse_parts.reshape(tok_local, -1), 'uly', split_axis=1, con...  4.41 us
    another operation x4, local copies, waits for them, and re-layouts  4.25 us
    unnamed x16, local copies, waits for them, and re-layouts  3.91 us
  transfers between devices with their start and end apart: 15, of which 7 were waited for; matrix products, arithmetic and copies ran while one was open for 22% of the time, Pallas kernels for 0%

commit v1 on v0

--- a/solution.py
+++ b/solution.py
@@ -9,6 +9,13 @@
 KEY_VALUE_HEADS = 8
 HOPS = 2
 QBLOCK = 512
+
+
+def exchange_blocks(x, name, split, join):
+    size = lax.axis_size(name)
+    shards = jnp.stack(jnp.split(x, size, axis=split), axis=0)
+    shards = lax.all_to_all(shards, name, split_axis=0, concat_axis=0)
+    return jnp.concatenate(shards, axis=join)
 
 
 def from_behind(block, axis, distance):
@@ -158,7 +165,7 @@
     query_total = query_acc.reshape(row_count, -1).astype(jnp.bfloat16)
     query_grad, key_grad, value_grad = (
         lax.all_to_all(query_total, "uly", split_axis=0, concat_axis=1, tiled=True),
-        lax.all_to_all(key_total, "uly", split_axis=0, concat_axis=1, tiled=True),
+        exchange_blocks(key_total, "uly", 0, 1),
         lax.all_to_all(value_total, "uly", split_axis=0, concat_axis=1, tiled=True),
     )
     return (query_grad, key_grad, value_grad)

time: 149 us -> 154 us (1.034)
  waiting for transfers between devices: 56.8 us -> 60 us
    ppermute x6, waiting for transfers between devices: 32.8 us -> 35.5 us  [from_behind(): return lax.ppermute(block, axis, route)]
    reshape x1 -> x2, local copies, waits for them, and re-layouts: 0.37 us -> 2.68 us  [per_device(): query_quad = query_loc.reshape(row_count, kv_heads, group_width, HEAD_SIZE)]
    reshape x1, local copies, waits for them, and re-layouts: 0.21 us -> 2.06 us  [per_device(): value_gradient_running.reshape(row_count, -1) + returned[1]]
    unnamed x16 -> x17, local copies, waits for them, and re-layouts: 3.91 us -> 2.1 us
    another operation x4 -> x5, local copies, waits for them, and re-layouts: 4.25 us -> 4.29 us
  transfers between devices with their start and end apart: 15 -> 15, of which waited for: 7 -> 9; matrix products, arithmetic and copies ran while one was open for 22% -> 23% of each run, Pallas kernels for 0% -> 0%
where the time goes in v1:
time: 154 us; the launch traced here: 153 us
  waiting for transfers between devices  60 us (39%)
  starting transfers between devices  47.8 us (31%)
  local copies, waits for them, and re-layouts  24.7 us (16%)
  other arithmetic  6.46 us (4%)
  blocking collectives  5.24 us (3%)
  matrix products  5.24 us (3%)
  between operations  3.64 us (2%)
    ppermute x6, waiting for transfers between devices, from_behind(): return lax.ppermute(block, axis, route)  35.5 us
    ppermute x6, starting transfers between devices, from_behind(): return lax.ppermute(block, axis, route)  15 us
    all_to_all x1, waiting for transfers between devices, per_device(): lax.all_to_all(query_inputs, 'uly', split_axis=1, concat_axis=0, tiled=True)  8.14 us
    all_gather x1, blocking collectives, per_device(): ids_loc = lax.all_gather(segment_ids, 'uly', axis=0, tiled=True)  5.24 us
    all_to_all x1, waiting for transfers between devices, exchange_blocks(): shards = lax.all_to_all(shards, name, split_axis=0, concat_axis=0)  4.77 us
    all_to_all x1, starting transfers between devices, per_device(): lax.all_to_all(lse_parts.reshape(tok_local, -1), 'uly', split_axis=1, con...  4.41 us
    another operation x4, local copies, waits for them, and re-layouts  4.27 us
    all_to_all x1, starting transfers between devices, per_device(): lax.all_to_all(query_inputs, 'uly', split_axis=1, concat_axis=0, tiled=True)  4.2 us
  transfers between devices with their start and end apart: 15, of which 9 were waited for; matrix products, arithmetic and copies ran while one was open for 23% of the time, Pallas kernels for 0%

profile of v1, /device:TPU:0, one launch (start us, length us, event | category | flops | bytes accessed | tf_op | source)
XLA Modules:
  0.0 153.1 jit_solution(10654347679116083511)
XLA Ops:
  0.7 4.4 %all-to-all-start.2 = ((f32[128,2,16]{0,2,1:T(8,128)}), f32[128,2,16]{0,2,1:T(8,128)S(1)}, u32[]{:S(2)}, u32[]{:S(2)}) async-start(f32[128,2,16]{0,2,1:T(8,128)} %bitcast.248), calls=%async_computation.2 | async-start | bytes 32768 | tf_op jit(solution)/shard_map/all_to_all | solution.py:78
  5.1 1.7 %copy.283 = bf16[16,2,8,512]{3,2,0,1:T(8,128)(2,1)} copy(bf16[16,2,8,512]{3,2,1,0:T(8,128)(2,1)} %bitcast.234) | data formatting | bytes 524288 | tf_op jit(solution)/shard_map/all_to_all | solution.py:74
  6.8 2.1 %all-to-all-done.2 = f32[128,2,16]{0,2,1:T(8,128)S(1)} async-done(((f32[128,2,16]{0,2,1:T(8,128)}), f32[128,2,16]{0,2,1:T(8,128)S(1)}, u32[]{:S(2)}, u32[]{:S(2)}) %all-to-all-start.2) | async-done | bytes 16416 | tf_op jit(solution)/shard_map/all_to_all | solution.py:78
  8.9 3.4 %all-to-all-start = ((bf16[128,2,512]{2,0,1:T(8,128)(2,1)}), bf16[128,2,512]{2,0,1:T(8,128)(2,1)S(1)}, u32[]{:S(2)}, u32[]{:S(2)}) async-start(bf16[128,2,512]{2,0,1:T(8,128)(2,1)} %bitcast.204), calls=%async_computation | async-start | bytes 524288 | tf_op jit(solution)/shard_map/all_to_all | solution.py:74
  12.4 1.7 %copy.282 = bf16[16,2,8,512]{3,2,0,1:T(8,128)(2,1)} copy(bf16[16,2,8,512]{3,2,1,0:T(8,128)(2,1)} %bitcast.235) | data formatting | bytes 524288 | tf_op jit(solution)/shard_map/all_to_all | solution.py:75
  14.1 3.4 %all-to-all-done = bf16[128,2,512]{2,0,1:T(8,128)(2,1)S(1)} async-done(((bf16[128,2,512]{2,0,1:T(8,128)(2,1)}), bf16[128,2,512]{2,0,1:T(8,128)(2,1)S(1)}, u32[]{:S(2)}, u32[]{:S(2)}) %all-to-all-start) | async-done | bytes 262176 | tf_op jit(solution)/shard_map/all_to_all | solution.py:74
  17.5 3.4 %all-to-all-start.3 = ((bf16[128,2,512]{2,0,1:T(8,128)(2,1)}), bf16[128,2,512]{2,0,1:T(8,128)(2,1)S(1)}, u32[]{:S(2)}, u32[]{:S(2)}) async-start(bf16[128,2,512]{2,0,1:T(8,128)(2,1)} %bitcast.203), calls=%async_computation.3 | async-start | bytes 524288 | tf_op jit(solution)/shard_map/all_to_all | solution.py:75
  21.0 5.2 %all-gather = s32[2,1,128]{2,1,0:T(1,128)S(1)} all-gather(s32[1,1,128]{2,1,0:T(1,128)S(1)} %bitcast.254), channel_id=1, replica_groups=mesh['uly'=2,'blk'=16] {'uly'}, dimensions={0}, use_global_device_ids=true | all-gather | bytes 1536 | tf_op jit(solution)/shard_map/all_gather | solution.py:83
  27.5 4.5 %collective-permute-start.2 = (s32[256]{0:T(256)S(1)}, s32[256]{0:T(256)S(1)}, u32[]{:S(2)}, u32[]{:S(2)}) collective-permute-start(s32[256]{0:T(256)S(1)} %bitcast.243), channel_id=1, source_target_pairs={{0,2},{1,3},{2,4},{3,5},{4,6},{5,7},{6,8},{7,9},{8,10},{9,11},{10,... | collective-permute-start | bytes 3080 | tf_op jit(solution)/shard_map/ppermute | solution.py:24
  32.8 3.5 %all-to-all-start.4 = ((bf16[128,2,1024]{2,0,1:T(8,128)(2,1)}), bf16[128,2,1024]{2,0,1:T(8,128)(2,1)S(1)}, u32[]{:S(2)}, u32[]{:S(2)}) async-start(bf16[128,2,1024]{2,0,1:T(8,128)(2,1)} %bitcast.201), calls=%async_computation.4 | async-start | bytes 1048576 | tf_op jit(solution)/shard_map/all_to_all | solution.py:73
  42.6 2.7 %all-to-all-done.4 = bf16[128,2,1024]{2,0,1:T(8,128)(2,1)S(1)} async-done(((bf16[128,2,1024]{2,0,1:T(8,128)(2,1)}), bf16[128,2,1024]{2,0,1:T(8,128)(2,1)S(1)}, u32[]{:S(2)}, u32[]{:S(2)}) %all-to-all-start.4) | async-done | bytes 524320 | tf_op jit(solution)/shard_map/all_to_all | solution.py:73
  45.3 3.5 %all-to-all-start.5 = ((bf16[128,2,1024]{2,0,1:T(8,128)(2,1)}), bf16[128,2,1024]{2,0,1:T(8,128)(2,1)S(1)}, u32[]{:S(2)}, u32[]{:S(2)}) async-start(bf16[128,2,1024]{2,0,1:T(8,128)(2,1)} %bitcast.200), calls=%async_computation.5 | async-start | bytes 1048576 | tf_op jit(solution)/shard_map/all_to_all | solution.py:76
  49.9 2.9 %collective-permute-start.1 = (bf16[2,256,512]{1,2,0:T(8,128)(2,1)}, bf16[2,256,512]{1,2,0:T(8,128)(2,1)}, u32[]{:S(2)}, u32[]{:S(2)}) collective-permute-start(bf16[2,256,512]{1,2,0:T(8,128)(2,1)} %pad_maximum_fusion.2), channel_id=1, source_target_pairs={{0,1},{1,2},{2,3},{3,4},{4,5},{5,6},{6,7},{7,8},{8,9},{9,10},{10,1... | collective-permute-start | bytes 1572872 | tf_op jit(solution)/shard_map/ppermute | solution.py:24
  52.9 3.4 %collective-permute-start.3 = (bf16[2,256,512]{1,2,0:T(8,128)(2,1)}, bf16[2,256,512]{1,2,0:T(8,128)(2,1)}, u32[]{:S(2)}, u32[]{:S(2)}) collective-permute-start(bf16[2,256,512]{1,2,0:T(8,128)(2,1)} %pad_maximum_fusion.2), channel_id=1, source_target_pairs={{0,2},{1,3},{2,4},{3,5},{4,6},{5,7},{6,8},{7,9},{8,10},{9,11},{10,... | collective-permute-start | bytes 1572872 | tf_op jit(solution)/shard_map/ppermute | solution.py:24
  57.4 4.2 %all-to-all-start.1 = ((bf16[128,2,1024]{2,0,1:T(8,128)(2,1)}), bf16[128,2,1024]{2,0,1:T(8,128)(2,1)}, u32[]{:S(2)}, u32[]{:S(2)}) async-start(bf16[128,2,1024]{2,0,1:T(8,128)(2,1)} %bitcast.202), calls=%async_computation.1 | async-start | bytes 1048576 | tf_op jit(solution)/shard_map/all_to_all | solution.py:72
  62.8 8.1 %all-to-all-done.1 = bf16[128,2,1024]{2,0,1:T(8,128)(2,1)} async-done(((bf16[128,2,1024]{2,0,1:T(8,128)(2,1)}), bf16[128,2,1024]{2,0,1:T(8,128)(2,1)}, u32[]{:S(2)}, u32[]{:S(2)}) %all-to-all-start.1) | async-done | bytes 524320 | tf_op jit(solution)/shard_map/all_to_all | solution.py:72
  71.0 1.4 reshape.109
  73.6 1.6 %fusion.19 = f32[4,2,256,256]{2,3,1,0:T(8,128)S(1)} fusion(bf16[256,4,2,128]{0,3,2,1:T(8,128)(2,1)} %copy.202, f32[4,2,256]{2,1,0:T(2,128)S(1)} %bitcast.249, pred[256,256]{0,1:T(8,128)(4,1)S(1)} %fusion.28, bf16[256,4,128,1]{2,1,0,3:T(4,128)(2,1)S(1)} %bitcast.219), kind=kOutput, calls=%fused_computation.33 | convolution fusion | flops 135790592 | bytes 2957312 | tf_op jit(solution)/shard_map/mhgd,nhd->hgmn/dot_general | solution.py:41
  76.8 2.1 %reshape.117 = f32[2,128,512]{2,1,0:T(8,128)} reshape(f32[256,4,128]{2,1,0:T(4,128)} %copy.205) | data formatting | bytes 1048576 | tf_op jit(solution)/shard_map/reshape | solution.py:164
  78.9 2.2 %conditional.2 = (f32[256,4,2,128]{3,0,2,1:T(8,128)}, f32[2,256,512]{1,2,0:T(8,128)}) conditional(s32[]{:T(128)} %convert_element_type.55, () %tuple.24, (s32[256]{0:T(256)S(1)}, s32[256]{0:T(256)S(1)}, bf16[2,256,512]{1,2,0:T(8,128)(2,1)}, bf16[256,4,2,128]{3,2,1,0:T(2,128)(2,1)S(1)}, f32[4,2,256,1]{2,1,0,3:T(2,128)S(1)}, ...), branch_computations={%region_3.4_spmd, %region_4.5_spmd} | conditional | flops 675479552 | bytes 33441920 | solution.py:157
  81.1 1.3 collective-permute-start.4
  82.4 2.1 %conditional.3 = (f32[256,4,2,128]{3,0,2,1:T(8,128)}, f32[2,256,512]{1,2,0:T(8,128)}) conditional(s32[]{:T(128)} %convert_element_type.56, () %tuple.26, (s32[256]{0:T(256)S(1)}, s32[256]{0:T(256)S(1)}, bf16[2,256,512]{1,2,0:T(8,128)(2,1)}, bf16[256,4,2,128]{3,2,1,0:T(2,128)(2,1)S(1)}, f32[4,2,256,1]{2,1,0,3:T(2,128)S(1)}, ...), branch_computations={%region_5.6_spmd, %region_6.7_spmd} | conditional | flops 675479552 | bytes 31344740 | solution.py:157
  84.5 1.6 %collective-permute-start.5 = (f32[2,256,512]{1,2,0:T(8,128)}, f32[2,256,512]{1,2,0:T(8,128)}, u32[]{:S(2)}, u32[]{:S(2)}) collective-permute-start(f32[2,256,512]{1,2,0:T(8,128)} %get-tuple-element.62), channel_id=1, source_target_pairs={{2,0},{3,1},{4,2},{5,3},{6,4},{7,5},{8,6},{9,7},{10,8},{11,9},{12,... | collective-permute-start | bytes 3145736 | tf_op jit(solution)/shard_map/ppermute | solution.py:24
  86.1 1.4 fusion.17
  89.3 1.7 %add_convert_fusion = bf16[256,4,2,128]{3,0,2,1:T(8,128)(2,1)S(1)} fusion(f32[256,4,2,128]{3,0,2,1:T(8,128)} %get-tuple-element.60, f32[256,4,2,128]{3,0,2,1:T(8,128)S(1)} %fusion.20, f32[256,4,2,128]{3,0,2,1:T(8,128)} %get-tuple-element.59), kind=kLoop, calls=%fused_computation.41 | loop fusion | flops 786432 | bytes 3670016 | tf_op jit(solution)/shard_map/convert_element_type | solution.py:165
  92.7 3.5 %all-to-all-start.6 = ((bf16[2,128,1024]{2,1,0:T(8,128)(2,1)}), bf16[2,128,1024]{2,1,0:T(8,128)(2,1)S(1)}, u32[]{:S(2)}, u32[]{:S(2)}) async-start(bf16[2,128,1024]{2,1,0:T(8,128)(2,1)} %convert_element_type.58), calls=%async_computation.6 | async-start | bytes 1048576 | tf_op jit(solution)/shard_map/all_to_all | solution.py:167
  97.0 34.7 %collective-permute-done.5 = f32[2,256,512]{1,2,0:T(8,128)} collective-permute-done((f32[2,256,512]{1,2,0:T(8,128)}, f32[2,256,512]{1,2,0:T(8,128)}, u32[]{:S(2)}, u32[]{:S(2)}) %collective-permute-start.5) | collective-permute-done | bytes 1048608 | tf_op jit(solution)/shard_map/ppermute | solution.py:24
  131.7 1.7 %add.27 = f32[2,256,512]{1,2,0:T(8,128)S(1)} add(f32[2,256,512]{1,2,0:T(8,128)} %collective-permute-done.4, f32[2,256,512]{1,2,0:T(8,128)} %collective-permute-done.5) | non-fusion elementwise | flops 262144 | bytes 3145728 | tf_op jit(solution)/shard_map/add | solution.py:162
  134.5 3.4 %all-to-all-start.7 = ((bf16[2,128,512]{1,2,0:T(8,128)(2,1)}), bf16[2,128,512]{1,2,0:T(8,128)(2,1)S(1)}, u32[]{:S(2)}, u32[]{:S(2)}) async-start(bf16[2,128,512]{1,2,0:T(8,128)(2,1)} %pad_maximum_fusion.3), calls=%async_computation.7 | async-start | bytes 524288 | tf_op jit(solution)/shard_map/all_to_all | solution.py:17
  138.7 4.8 %all-to-all-done.7 = bf16[2,128,512]{1,2,0:T(8,128)(2,1)S(1)} async-done(((bf16[2,128,512]{1,2,0:T(8,128)(2,1)}), bf16[2,128,512]{1,2,0:T(8,128)(2,1)S(1)}, u32[]{:S(2)}, u32[]{:S(2)}) %all-to-all-start.7) | async-done | bytes 262176 | tf_op jit(solution)/shard_map/all_to_all | solution.py:17
  143.5 3.4 %all-to-all-start.8 = ((bf16[2,128,512]{2,1,0:T(8,128)(2,1)}), bf16[2,128,512]{2,1,0:T(8,128)(2,1)S(1)}, u32[]{:S(2)}, u32[]{:S(2)}) async-start(bf16[2,128,512]{2,1,0:T(8,128)(2,1)} %add_convert_fusion.1), calls=%async_computation.8 | async-start | bytes 524288 | tf_op jit(solution)/shard_map/all_to_all | solution.py:169
  149.1 3.0 %all-to-all-done.8 = bf16[2,128,512]{2,1,0:T(8,128)(2,1)S(1)} async-done(((bf16[2,128,512]{2,1,0:T(8,128)(2,1)}), bf16[2,128,512]{2,1,0:T(8,128)(2,1)S(1)}, u32[]{:S(2)}, u32[]{:S(2)}) %all-to-all-start.8) | async-done | bytes 262176 | tf_op jit(solution)/shard_map/all_to_all | solution.py:169
  (69 shorter events, 25.4 us)
Async XLA Ops:
  0.6 20.4 %copy-start.13 = (s32[128]{0:T(128)S(1)}, s32[128]{0:T(128)}, u32[]{:S(2)}) copy-start(s32[128]{0:T(128)} %param.17) | copy-start | bytes 1540
  0.6 31.4 %copy-start.10 = (bf16[128,2048]{1,0:T(8,128)(2,1)S(1)}, bf16[128,2048]{1,0:T(8,128)(2,1)}, u32[]{:S(2)}) copy-start(bf16[128,2048]{1,0:T(8,128)(2,1)} %param.15) | copy-start | bytes 1572868
  0.7 8.3 %all-to-all-start.2 = ((f32[128,2,16]{0,2,1:T(8,128)}), f32[128,2,16]{0,2,1:T(8,128)S(1)}, u32[]{:S(2)}, u32[]{:S(2)}) async-start(f32[128,2,16]{0,2,1:T(8,128)} %bitcast.248), calls=%async_computation.2 | async-start | bytes 32768 | tf_op jit(solution)/shard_map/all_to_all | solution.py:78
  5.1 31.9 %copy-start.11 = (bf16[128,2048]{1,0:T(8,128)(2,1)S(1)}, bf16[128,2048]{1,0:T(8,128)(2,1)}, u32[]{:S(2)}) copy-start(bf16[128,2048]{1,0:T(8,128)(2,1)} %param.14) | copy-start | bytes 1572868
  8.9 8.6 %all-to-all-start = ((bf16[128,2,512]{2,0,1:T(8,128)(2,1)}), bf16[128,2,512]{2,0,1:T(8,128)(2,1)S(1)}, u32[]{:S(2)}, u32[]{:S(2)}) async-start(bf16[128,2,512]{2,0,1:T(8,128)(2,1)} %bitcast.204), calls=%async_computation | async-start | bytes 524288 | tf_op jit(solution)/shard_map/all_to_all | solution.py:74
  12.4 25.4 %copy-start.12 = (bf16[128,2048]{1,0:T(8,128)(2,1)S(1)}, bf16[128,2048]{1,0:T(8,128)(2,1)}, u32[]{:S(2)}) copy-start(bf16[128,2048]{1,0:T(8,128)(2,1)} %param.11) | copy-start | bytes 1572868
  17.5 15.3 %all-to-all-start.3 = ((bf16[128,2,512]{2,0,1:T(8,128)(2,1)}), bf16[128,2,512]{2,0,1:T(8,128)(2,1)S(1)}, u32[]{:S(2)}, u32[]{:S(2)}) async-start(bf16[128,2,512]{2,0,1:T(8,128)(2,1)} %bitcast.203), calls=%async_computation.3 | async-start | bytes 524288 | tf_op jit(solution)/shard_map/all_to_all | solution.py:75
  26.2 12.4 %collective-permute-start = (s32[256]{0:T(256)S(1)}, s32[256]{0:T(256)S(1)}, u32[]{:S(2)}, u32[]{:S(2)}) collective-permute-start(s32[256]{0:T(256)S(1)} %bitcast.242), channel_id=1, source_target_pairs={{0,1},{1,2},{2,3},{3,4},{4,5},{5,6},{6,7},{7,8},{8,9},{9,10},{10,1... | collective-permute-start | bytes 3080 | tf_op jit(solution)/shard_map/ppermute | solution.py:24
  27.5 13.0 %collective-permute-start.2 = (s32[256]{0:T(256)S(1)}, s32[256]{0:T(256)S(1)}, u32[]{:S(2)}, u32[]{:S(2)}) collective-permute-start(s32[256]{0:T(256)S(1)} %bitcast.243), channel_id=1, source_target_pairs={{0,2},{1,3},{2,4},{3,5},{4,6},{5,7},{6,8},{7,9},{8,10},{9,11},{10,... | collective-permute-start | bytes 3080 | tf_op jit(solution)/shard_map/ppermute | solution.py:24
  32.8 12.5 %all-to-all-start.4 = ((bf16[128,2,1024]{2,0,1:T(8,128)(2,1)}), bf16[128,2,1024]{2,0,1:T(8,128)(2,1)S(1)}, u32[]{:S(2)}, u32[]{:S(2)}) async-start(bf16[128,2,1024]{2,0,1:T(8,128)(2,1)} %bitcast.201), calls=%async_computation.4 | async-start | bytes 1048576 | tf_op jit(solution)/shard_map/all_to_all | solution.py:73
  45.3 12.1 %all-to-all-start.5 = ((bf16[128,2,1024]{2,0,1:T(8,128)(2,1)}), bf16[128,2,1024]{2,0,1:T(8,128)(2,1)S(1)}, u32[]{:S(2)}, u32[]{:S(2)}) async-start(bf16[128,2,1024]{2,0,1:T(8,128)(2,1)} %bitcast.200), calls=%async_computation.5 | async-start | bytes 1048576 | tf_op jit(solution)/shard_map/all_to_all | solution.py:76
  49.9 29.0 %collective-permute-start.1 = (bf16[2,256,512]{1,2,0:T(8,128)(2,1)}, bf16[2,256,512]{1,2,0:T(8,128)(2,1)}, u32[]{:S(2)}, u32[]{:S(2)}) collective-permute-start(bf16[2,256,512]{1,2,0:T(8,128)(2,1)} %pad_maximum_fusion.2), channel_id=1, source_target_pairs={{0,1},{1,2},{2,3},{3,4},{4,5},{5,6},{6,7},{7,8},{8,9},{9,10},{10,1... | collective-permute-start | bytes 1572872 | tf_op jit(solution)/shard_map/ppermute | solution.py:24
  52.9 29.5 %collective-permute-start.3 = (bf16[2,256,512]{1,2,0:T(8,128)(2,1)}, bf16[2,256,512]{1,2,0:T(8,128)(2,1)}, u32[]{:S(2)}, u32[]{:S(2)}) collective-permute-start(bf16[2,256,512]{1,2,0:T(8,128)(2,1)} %pad_maximum_fusion.2), channel_id=1, source_target_pairs={{0,2},{1,3},{2,4},{3,5},{4,6},{5,7},{6,8},{7,9},{8,10},{9,11},{10,... | collective-permute-start | bytes 1572872 | tf_op jit(solution)/shard_map/ppermute | solution.py:24
  57.4 13.5 %all-to-all-start.1 = ((bf16[128,2,1024]{2,0,1:T(8,128)(2,1)}), bf16[128,2,1024]{2,0,1:T(8,128)(2,1)}, u32[]{:S(2)}, u32[]{:S(2)}) async-start(bf16[128,2,1024]{2,0,1:T(8,128)(2,1)} %bitcast.202), calls=%async_computation.1 | async-start | bytes 1048576 | tf_op jit(solution)/shard_map/all_to_all | solution.py:72
  81.1 16.0 %collective-permute-start.4 = (f32[2,256,512]{1,2,0:T(8,128)}, f32[2,256,512]{1,2,0:T(8,128)}, u32[]{:S(2)}, u32[]{:S(2)}) collective-permute-start(f32[2,256,512]{1,2,0:T(8,128)} %get-tuple-element.61), channel_id=1, source_target_pairs={{1,0},{2,1},{3,2},{4,3},{5,4},{6,5},{7,6},{8,7},{9,8},{10,9},{11,1... | collective-permute-start | bytes 3145736 | tf_op jit(solution)/shard_map/ppermute | solution.py:24
  84.5 3.0 %copy-start.4 = (bf16[256,4,2,128]{0,3,2,1:T(8,128)(2,1)S(1)}, bf16[256,4,2,128]{0,3,2,1:T(8,128)(2,1)}, u32[]{:S(2)}) copy-start(bf16[256,4,2,128]{0,3,2,1:T(8,128)(2,1)} %copy.202) | copy-start | bytes 1572868
  84.5 47.2 %collective-permute-start.5 = (f32[2,256,512]{1,2,0:T(8,128)}, f32[2,256,512]{1,2,0:T(8,128)}, u32[]{:S(2)}, u32[]{:S(2)}) collective-permute-start(f32[2,256,512]{1,2,0:T(8,128)} %get-tuple-element.62), channel_id=1, source_target_pairs={{2,0},{3,1},{4,2},{5,3},{6,4},{7,5},{8,6},{9,7},{10,8},{11,9},{12,... | collective-permute-start | bytes 3145736 | tf_op jit(solution)/shard_map/ppermute | solution.py:24
  92.7 41.8 %all-to-all-start.6 = ((bf16[2,128,1024]{2,1,0:T(8,128)(2,1)}), bf16[2,128,1024]{2,1,0:T(8,128)(2,1)S(1)}, u32[]{:S(2)}, u32[]{:S(2)}) async-start(bf16[2,128,1024]{2,1,0:T(8,128)(2,1)} %convert_element_type.58), calls=%async_computation.6 | async-start | bytes 1048576 | tf_op jit(solution)/shard_map/all_to_all | solution.py:167
  96.2 37.2 %copy-start.5 = (f32[4,256,128]{1,2,0:T(8,128)S(1)}, f32[4,256,128]{1,2,0:T(8,128)}, u32[]{:S(2)}) copy-start(f32[4,256,128]{1,2,0:T(8,128)} %fusion.21) | copy-start | bytes 1572868
  133.4 4.5 %copy-start.3 = (f32[2,128,512]{2,1,0:T(8,128)S(1)}, f32[2,128,512]{2,1,0:T(8,128)}, u32[]{:S(2)}) copy-start(f32[2,128,512]{2,1,0:T(8,128)} %reshape.117) | copy-start | bytes 1572868
  134.5 9.0 %all-to-all-start.7 = ((bf16[2,128,512]{1,2,0:T(8,128)(2,1)}), bf16[2,128,512]{1,2,0:T(8,128)(2,1)S(1)}, u32[]{:S(2)}, u32[]{:S(2)}) async-start(bf16[2,128,512]{1,2,0:T(8,128)(2,1)} %pad_maximum_fusion.3), calls=%async_computation.7 | async-start | bytes 524288 | tf_op jit(solution)/shard_map/all_to_all | solution.py:17
  143.5 8.6 %all-to-all-start.8 = ((bf16[2,128,512]{2,1,0:T(8,128)(2,1)}), bf16[2,128,512]{2,1,0:T(8,128)(2,1)S(1)}, u32[]{:S(2)}, u32[]{:S(2)}) async-start(bf16[2,128,512]{2,1,0:T(8,128)(2,1)} %add_convert_fusion.1), calls=%async_computation.8 | async-start | bytes 524288 | tf_op jit(solution)/shard_map/all_to_all | solution.py:169
